TPU v7x, 256 devices: a whole 4x4x8 slice. The times are simulated.
256 devices in a mesh: dp: 8 (over x, z_hi), ts: 32 (over z_lo, y, core).
Axes of the slice: x: 4, y: 4, z: 8 (z_hi: 2, z_lo: 4; z = z_hi * 4 + z_lo), core: 2. Of those that a mesh axis runs over, the one named last changes fastest.
Arguments:
- clip_video: bfloat16 [512, 4, 40, 128], P(('dp', 'ts')), may hold values from -6 to 6
- conv_weight: bfloat16 [3, 3, 3, 128, 128], replicated, may hold values from -0.109375 to 0.109375
- embed_weight: bfloat16 [128, 5120], replicated, may hold values from -0.5 to 0.5
- gain_spatial: float32 [5120], replicated, may hold values from 0.5 to 1.5
- gain_temporal: float32 [5120], replicated, may hold values from 0.5 to 1.5
- input_spatial: bfloat16 [5120, 384], P(('dp', 'ts')), may hold values from -0.078125 to 0.078125
- input_temporal: bfloat16 [5120, 384], P(('dp', 'ts')), may hold values from -0.078125 to 0.078125
- output_spatial: bfloat16 [128, 5120], replicated, may hold values from -2 to 2
- output_temporal: bfloat16 [128, 5120], replicated, may hold values from -2 to 2
- cotangent: bfloat16 [512, 4, 40, 5120], P(('dp', 'ts')), may hold values from -6 to 6
Outputs:
- layer_output: bfloat16 [512, 4, 40, 5120], P(('dp', 'ts'))
- grad_spatial: float32 [5120, 384], P(('dp', 'ts'))
All inputs are finite; a program needn't handle non-finite values.
Results may differ from a plain program's by a relative error of at most 0.015.
Values may be sent and summed in bfloat16 or wider, within the bound.
No kernel may reach another device: no remote copies, remote signals or barrier semaphores. Data moves between devices by JAX's collectives and lax.ppermute only.
A program may use at most 128 MiB of HBM per device.

v0:
```python
import jax
import jax.numpy as jnp
from jax import lax
from jax.sharding import PartitionSpec as P

FR = 16
epsilon = 1e-06
masked = -1e30


def passed_along(block, axis, distance):
    devices = range(lax.axis_size(axis))
    route = [(i - distance, i) for i in devices if i - distance in devices]
    return lax.ppermute(block, axis, route)


def side_by_side(arrays, axis, dim, along):
    widths = [a.shape[along] for a in arrays]
    both = jnp.concatenate(arrays, axis=along)
    whole = lax.all_gather(both, axis, axis=dim, tiled=True)
    return tuple(jnp.split(whole, [sum(widths[:k]) for k in range(1, len(widths))], axis=along))


def in_blocks(value, dim, size):
    dims = value.shape
    parts = value.reshape(*dims[:dim], size, dims[dim] // size, *dims[dim + 1 :])
    return jnp.moveaxis(parts, dim, 0)


def sum_at_owner(value, axis, dim):
    parts = in_blocks(value, dim, lax.axis_size(axis))
    arrived = lax.all_to_all(parts, axis, split_axis=0, concat_axis=0, tiled=True)
    return arrived.astype(jnp.float32).sum(axis=0)


def conv_local(volume, weight, count):
    frames, height, columns, channels = volume.shape
    out_channels = weight.shape[-1]
    padded = jnp.pad(volume, ((0, 0), (1, 1), (1, 1), (0, 0)))
    summed = jnp.zeros((count * height * columns, out_channels), jnp.float32)
    for time_tap in range(3):
        for row_tap in range(3):
            for col_tap in range(3):
                window = padded[
                    2 - time_tap : 2 - time_tap + count,
                    row_tap : row_tap + height,
                    col_tap : col_tap + columns,
                    :,
                ]
                summed = summed + jnp.dot(
                    window.reshape(-1, channels),
                    weight[time_tap, row_tap, col_tap],
                    preferred_element_type=jnp.float32,
                )
    return summed.reshape(count, height, columns, out_channels)


def rms_norm(hidden, norm_gain):
    widened = hidden.astype(jnp.float32)
    factor = lax.rsqrt(jnp.mean(widened * widened, axis=-1, keepdims=True) + epsilon)
    return ((widened * factor * norm_gain).astype(jnp.bfloat16), factor)


def rms_norm_grad(hidden, norm_gain, factor, upstream):
    widened = hidden.astype(jnp.float32)
    scaled = upstream * norm_gain
    inner_mean = jnp.mean(widened * scaled, axis=-1, keepdims=True)
    return factor * scaled - widened * factor**3 * inner_mean


def frame_forward(packed):
    frames, places, triple = packed.shape
    head_size = triple // 3
    queries = packed[..., :head_size]
    key_rows = packed[..., head_size : 2 * head_size]
    values = packed[..., 2 * head_size :]
    scores = jnp.einsum(
        "fqd,fkd->fqk", queries, key_rows, preferred_element_type=jnp.float32
    ) * head_size ** (-0.5)
    attend = jax.nn.softmax(scores, axis=-1)
    rounded = attend.astype(jnp.bfloat16)
    mixture = jnp.einsum("fqk,fkd->fqd", rounded, values, preferred_element_type=jnp.float32)
    return (mixture.astype(jnp.bfloat16), attend)


def frame_backward(packed, attend, upstream):
    frames, places, triple = packed.shape
    head_size = triple // 3
    scale_factor = head_size ** (-0.5)
    queries = packed[..., :head_size]
    key_rows = packed[..., head_size : 2 * head_size]
    values = packed[..., 2 * head_size :]
    rounded = attend.astype(jnp.bfloat16)
    grad_attend = jnp.einsum("fqd,fkd->fqk", upstream, values, preferred_element_type=jnp.float32)
    grad_values = jnp.einsum("fqk,fqd->fkd", rounded, upstream, preferred_element_type=jnp.float32)
    grad_scores = attend * (grad_attend - jnp.sum(grad_attend * attend, axis=-1, keepdims=True))
    grad_rounded = grad_scores.astype(jnp.bfloat16)
    grad_queries = (
        jnp.einsum("fqk,fkd->fqd", grad_rounded, key_rows, preferred_element_type=jnp.float32)
        * scale_factor
    )
    grad_keys = (
        jnp.einsum("fqk,fqd->fkd", grad_rounded, queries, preferred_element_type=jnp.float32)
        * scale_factor
    )
    joined = jnp.concatenate([grad_queries, grad_keys, grad_values], axis=-1)
    return joined.astype(jnp.bfloat16)


def clip_forward(packed):
    frames, places, triple = packed.shape
    head_size = triple // 3
    volume = packed.reshape(frames // FR, FR, places, triple)
    queries = volume[..., :head_size]
    key_rows = volume[..., head_size : 2 * head_size]
    values = volume[..., 2 * head_size :]
    scores = jnp.einsum(
        "cqpd,ckpd->cpqk", queries, key_rows, preferred_element_type=jnp.float32
    ) * head_size ** (-0.5)
    allowed = jnp.arange(FR)[:, None] >= jnp.arange(FR)[None, :]
    scores = jnp.where(allowed, scores, masked)
    attend = jax.nn.softmax(scores, axis=-1)
    rounded = attend.astype(jnp.bfloat16)
    mixture = jnp.einsum("cpqk,ckpd->cqpd", rounded, values, preferred_element_type=jnp.float32)
    return (mixture.astype(jnp.bfloat16).reshape(frames, places, head_size), attend)


def clip_backward(packed, attend, upstream):
    frames, places, triple = packed.shape
    head_size = triple // 3
    scale_factor = head_size ** (-0.5)
    volume = packed.reshape(frames // FR, FR, places, triple)
    queries = volume[..., :head_size]
    key_rows = volume[..., head_size : 2 * head_size]
    values = volume[..., 2 * head_size :]
    grad_out = upstream.reshape(frames // FR, FR, places, head_size)
    rounded = attend.astype(jnp.bfloat16)
    grad_attend = jnp.einsum(
        "cqpd,ckpd->cpqk", grad_out, values, preferred_element_type=jnp.float32
    )
    grad_values = jnp.einsum(
        "cpqk,cqpd->ckpd", rounded, grad_out, preferred_element_type=jnp.float32
    )
    grad_scores = attend * (grad_attend - jnp.sum(grad_attend * attend, axis=-1, keepdims=True))
    grad_rounded = grad_scores.astype(jnp.bfloat16)
    grad_queries = (
        jnp.einsum("cpqk,ckpd->cqpd", grad_rounded, key_rows, preferred_element_type=jnp.float32)
        * scale_factor
    )
    grad_keys = (
        jnp.einsum("cpqk,cqpd->ckpd", grad_rounded, queries, preferred_element_type=jnp.float32)
        * scale_factor
    )
    joined = jnp.concatenate([grad_queries, grad_keys, grad_values], axis=-1)
    return joined.astype(jnp.bfloat16).reshape(frames, places, triple)


def shards(
    clip_video,
    conv_weight,
    embed_weight,
    gain_spatial,
    gain_temporal,
    input_spatial,
    input_temporal,
    output_spatial,
    output_temporal,
    cotangent,
):
    frames_here = clip_video.shape[0]
    prior = passed_along(clip_video, "ts", 1)
    opening = lax.axis_index("ts") == 0
    prior = jnp.where(opening, jnp.zeros_like(prior), prior)
    volume = jnp.concatenate([prior, clip_video], axis=0)
    whole_spatial, whole_temporal = side_by_side(
        (input_spatial, input_temporal), ("dp", "ts"), 0, 1
    )
    features = jax.nn.gelu(conv_local(volume, conv_weight, frames_here), approximate=True).astype(
        jnp.bfloat16
    )
    frames, height, columns, channels = features.shape
    places = height * columns
    tokens = frames * places
    embedded = jnp.dot(
        features.reshape(tokens, channels), embed_weight, preferred_element_type=jnp.float32
    ).astype(jnp.bfloat16)
    normed_one, factor_one = rms_norm(embedded, gain_spatial)
    packed_one = jnp.dot(normed_one, whole_spatial, preferred_element_type=jnp.float32).astype(
        jnp.bfloat16
    )
    packed_one = packed_one.reshape(frames, places, -1)
    mixture_one, attend_one = frame_forward(packed_one)
    after_space = (
        embedded.astype(jnp.float32)
        + jnp.dot(
            mixture_one.reshape(tokens, -1), output_spatial, preferred_element_type=jnp.float32
        )
    ).astype(jnp.bfloat16)
    normed_two, factor_two = rms_norm(after_space, gain_temporal)
    packed_two = jnp.dot(normed_two, whole_temporal, preferred_element_type=jnp.float32).astype(
        jnp.bfloat16
    )
    packed_two = packed_two.reshape(frames, places, -1)
    cotangent_rows = cotangent.reshape(tokens, -1)
    grad_mix_two = jnp.dot(
        cotangent_rows, output_temporal.T, preferred_element_type=jnp.float32
    ).astype(jnp.bfloat16)
    grad_mix_two = grad_mix_two.reshape(frames, places, -1)
    patched = lax.all_to_all(packed_two, "ts", split_axis=1, concat_axis=0, tiled=True)
    mixture_patched, attend_two = clip_forward(patched)
    mixture_two = lax.all_to_all(mixture_patched, "ts", split_axis=0, concat_axis=1, tiled=True)
    grad_patched = lax.all_to_all(grad_mix_two, "ts", split_axis=1, concat_axis=0, tiled=True)
    grad_packed_patched = clip_backward(patched, attend_two, grad_patched)
    grad_packed_two = lax.all_to_all(
        grad_packed_patched, "ts", split_axis=0, concat_axis=1, tiled=True
    )
    after_time = (
        after_space.astype(jnp.float32)
        + jnp.dot(
            mixture_two.reshape(tokens, -1), output_temporal, preferred_element_type=jnp.float32
        )
    ).astype(jnp.bfloat16)
    grad_packed_two = grad_packed_two.reshape(tokens, -1)
    grad_normed_two = jnp.dot(grad_packed_two, whole_temporal.T, preferred_element_type=jnp.float32)
    grad_after = (
        cotangent_rows.astype(jnp.float32)
        + rms_norm_grad(after_space, gain_temporal, factor_two, grad_normed_two)
    ).astype(jnp.bfloat16)
    grad_mix_one = jnp.dot(grad_after, output_spatial.T, preferred_element_type=jnp.float32).astype(
        jnp.bfloat16
    )
    grad_packed_one = frame_backward(
        packed_one, attend_one, grad_mix_one.reshape(frames, places, -1)
    ).reshape(tokens, -1)
    part_spatial = lax.dot_general(
        normed_one, grad_packed_one, (((0,), (0,)), ((), ())), preferred_element_type=jnp.float32
    )
    group_spatial = lax.psum_scatter(
        part_spatial.astype(jnp.bfloat16), "dp", scatter_dimension=0, tiled=True
    )
    grad_spatial = sum_at_owner(group_spatial, "ts", 0)
    return (after_time.reshape(frames, height, columns, -1), grad_spatial)


def solution(mesh):
    placed = (
        P(("dp", "ts"), None, None, None),
        P(),
        P(),
        P(),
        P(),
        P(("dp", "ts"), None),
        P(("dp", "ts"), None),
        P(),
        P(),
        P(("dp", "ts"), None, None, None),
    )
    return jax.shard_map(
        shards,
        mesh=mesh,
        in_specs=placed,
        out_specs=(P(("dp", "ts"), None, None, None), P(("dp", "ts"), None)),
        check_vma=False,
    )
```

profile of v0, /device:TPU:1, one launch (start us, length us, event | category | flops | bytes accessed | tf_op | source)
XLA Modules:
  0.0 364.3 jit_solution(13691863951065526166)
XLA Ops:
  7.2 1.5 maximum_bitcast_fusion
  8.7 4.6 %collective-permute-start = (bf16[2,4,40,128]{3,2,1,0:T(8,128)(2,1)}, bf16[2,4,40,128]{3,2,1,0:T(8,128)(2,1)S(1)}, u32[]{:S(2)}, u32[]{:S(2)}) collective-permute-start(bf16[2,4,40,128]{3,2,1,0:T(8,128)(2,1)} %param.10), channel_id=1, source_target_pairs={{0,1},{1,2},{2,3},{3,4},{4,5},{5,6},{6,7},{7,8},{8,9},{9,10},{10,1... | collective-permute-start | bytes 245768 | tf_op jit(solution)/shard_map/ppermute | solution.py:14
  13.3 3.4 convolution_convert_fusion.2
  16.7 0.7 copy.45
  17.4 8.5 %all-to-all-start.2 = ((bf16[2,160,128]{2,0,1:T(2,128)(2,1)}), bf16[2,160,128]{2,0,1:T(2,128)(2,1)S(1)}, u32[]{:S(2)}, u32[]{:S(2)}) async-start(bf16[2,160,128]{2,0,1:T(2,128)(2,1)} %copy.45), calls=%async_computation.2 | async-start | bytes 163840 | tf_op jit(solution)/shard_map/all_to_all | solution.py:212
  26.1 0.2 pad_slice_fusion
  26.6 0.2 convolution_add_fusion.24
  26.8 0.2 convolution_add_fusion.23
  27.0 0.2 convolution_add_fusion.22
  27.1 0.2 convolution_add_fusion.21
  27.3 0.2 convolution_add_fusion.20
  27.5 0.2 convolution_add_fusion.19
  27.8 0.2 convolution_add_fusion.17
  27.9 0.2 convolution_add_fusion.16
  28.1 0.2 convolution_add_fusion.15
  28.3 0.2 convolution_add_fusion.14
  28.4 0.2 convolution_add_fusion.13
  28.6 0.2 convolution_add_fusion.12
  28.7 0.2 convolution_add_fusion.11
  28.9 0.2 convolution_add_fusion.10
  29.1 0.2 convolution_add_fusion.9
  29.2 0.2 convolution_add_fusion.8
  29.4 0.2 convolution_add_fusion.7
  29.5 0.2 convolution_add_fusion.6
  29.7 0.2 convolution_add_fusion.5
  29.9 0.2 convolution_add_fusion.4
  30.0 0.2 fusion.38
  30.2 0.2 convolution_add_fusion.2
  30.3 0.2 convolution_add_fusion.1
  30.5 4.2 %fusion.4 = (f32[320]{0:T(512)S(1)}, bf16[320,5120]{1,0:T(8,128)(2,1)}) fusion(bf16[128,5120]{1,0:T(8,128)(2,1)} %param.12, f32[320,128]{1,0:T(8,128)S(1)} %convolution_add_fusion.1, bf16[320,128]{1,0:T(8,128)(2,1)S(1)} %bitcast.244, bf16[3,3,3,128,128]{4,3,2,1,0:T(8,128)(2,1)S(1)} %copy-done.5), kind=kOutput, calls=%fused_computation.15 | convolution fusion | flops 436879040 | bytes 4867328 | tf_op jit(solution)/shard_map/dot_general | solution.py:184
  34.7 100.0 %all-gather.3.cloned.1.call-done = bf16[256,20,768]{2,1,0:T(8,128)(2,1)} async-done(((bf16[1,20,768]{2,1,0:T(8,128)(2,1)}), bf16[256,20,768]{2,1,0:T(8,128)(2,1)}) %all-gather.3.cloned.1.call-update) | async-done | bytes 7864336 | tf_op jit(solution)/shard_map/all_gather | solution.py:20
  134.7 12.5 %reshape.220 = bf16[5120,768]{1,0:T(8,128)(2,1)} reshape(bf16[256,20,768]{2,1,0:T(8,128)(2,1)} %all-gather.3.cloned.1.call-done) | data formatting | bytes 15728640
  147.2 5.0 %fusion.26 = bf16[320,384]{1,0:T(8,128)(2,1)S(1)} fusion(bf16[5120,768]{1,0:T(8,128)(2,1)} %reshape.220, bf16[320,5120]{1,0:T(8,128)(2,1)} %get-tuple-element.32, f32[5120]{0:T(1024)S(1)} %copy-done.8, f32[320]{0:T(512)S(1)} %add_rsqrt_fusion.1), kind=kOutput, calls=%fused_computation.35 | convolution fusion | flops 1264967680 | bytes 7476480 | tf_op jit(solution)/shard_map/dot_general | solution.py:188
  152.2 0.3 fusion.182
  152.5 0.5 convolution_convert_fusion.6
  153.0 3.3 fusion.7
  156.3 5.2 %fusion.29 = bf16[320,384]{1,0:T(8,128)(2,1)S(1)} fusion(bf16[5120,768]{1,0:T(8,128)(2,1)} %reshape.220, bf16[320,5120]{1,0:T(8,128)(2,1)S(1)} %get-tuple-element.36, f32[5120]{0:T(1024)S(1)} %copy-done.7, f32[320]{0:T(512)S(1)} %get-tuple-element.30), kind=kOutput, calls=%fused_computation.36 | convolution fusion | flops 1264967680 | bytes 7476480 | tf_op jit(solution)/shard_map/dot_general | solution.py:200
  161.5 0.9 copy.36
  162.4 7.1 %all-to-all-start = ((bf16[2,160,384]{2,0,1:T(2,128)(2,1)}), bf16[2,160,384]{2,0,1:T(2,128)(2,1)S(1)}, u32[]{:S(2)}, u32[]{:S(2)}) async-start(bf16[2,160,384]{2,0,1:T(2,128)(2,1)} %copy.36), calls=%async_computation | async-start | bytes 491520 | tf_op jit(solution)/shard_map/all_to_all | solution.py:209
  169.7 10.6 %all-to-all-done = bf16[2,160,384]{2,0,1:T(2,128)(2,1)S(1)} async-done(((bf16[2,160,384]{2,0,1:T(2,128)(2,1)}), bf16[2,160,384]{2,0,1:T(2,128)(2,1)S(1)}, u32[]{:S(2)}, u32[]{:S(2)}) %all-to-all-start) | async-done | bytes 245792 | tf_op jit(solution)/shard_map/all_to_all | solution.py:209
  180.3 0.2 copy.37
  180.6 0.2 fusion.37
  180.8 0.8 fusion.187
  181.6 0.2 fusion.47
  181.8 0.2 multiply_reduce_fusion.1
  182.0 0.2 fusion.48
  182.2 0.2 fusion.49
  182.6 17.4 %all_to_all.65 = bf16[64,5,384]{2,1,0:T(8,128)(2,1)S(1)} all-to-all(bf16[64,5,384]{2,1,0:T(8,128)(2,1)S(1)} %copy.53), channel_id=1, replica_groups=mesh['dp'=8,'ts'=32] {'ts'}, dimensions={0} | all-to-all | bytes 491520 | tf_op jit(solution)/shard_map/all_to_all | solution.py:214
  200.2 5.3 %fusion.14 = (f32[320]{0:T(512)S(1)}, f32[320,5120]{1,0:T(8,128)S(1)}) fusion(bf16[320,5120]{1,0:T(8,128)(2,1)} %copy-done.1, f32[5120]{0:T(1024)S(1)} %copy-done.7, bf16[320,384]{1,0:T(8,128)(2,1)S(1)} %reshape.216, bf16[5120,768]{1,0:T(8,128)(2,1)} %reshape.220), kind=kOutput, calls=%fused_computation.25 | convolution fusion | flops 1264844544 | bytes 14030080 | tf_op jit(solution)/shard_map/dot_general | solution.py:224
  205.5 2.0 fusion.41
  207.5 0.4 convolution_convert_fusion.4
  207.9 0.2 multiply_reduce_fusion
  208.2 0.2 fusion.40
  208.4 0.3 fusion.39
  208.6 6.6 %convolution_convert_fusion = bf16[5120,384]{1,0:T(8,128)(2,1)} fusion(bf16[320,5120]{1,0:T(8,128)(2,1)} %get-tuple-element.32, f32[5120]{0:T(1024)S(1)} %copy-done.8, f32[320]{0:T(512)S(1)} %add_rsqrt_fusion.1, bf16[320,128]{1,0:T(8,128)(2,1)S(1)} %bitcast.251, bf16[320,128]{1,0:T(8,128)(2,1)S(1)} %bitcast.252, bf16[320,128]{1,0:T(8,128)(2,1)S(1)} %bitcast.241), kind=kOutput, calls=%fused_computation.11 | convolution fusion | flops 1267548160 | bytes 7476480 | tf_op jit(solution)/shard_map/dot_general | solution.py:235
  215.3 0.2 fusion.46
  215.5 0.7 copy.43
  216.2 3.9 %all-to-all-start.1 = ((bf16[64,5,128]{2,1,0:T(8,128)(2,1)}), bf16[64,5,128]{2,1,0:T(8,128)(2,1)S(1)}, u32[]{:S(2)}, u32[]{:S(2)}) async-start(bf16[64,5,128]{2,1,0:T(8,128)(2,1)} %copy.43), calls=%async_computation.1 | async-start | bytes 262144 | tf_op jit(solution)/shard_map/all_to_all | solution.py:211
  220.2 109.8 %reduce-scatter.2.cloned.1.call-done = bf16[640,384]{1,0:T(8,128)(2,1)} async-done(((bf16[5120,384]{1,0:T(8,128)(2,1)}), bf16[640,384]{1,0:T(8,128)(2,1)}) %reduce-scatter.2.cloned.1.call-update) | async-done | bytes 491536 | tf_op jit(solution)/shard_map/reduce_scatter | solution.py:238
  330.0 1.9 reshape.218
  331.9 7.1 %all-to-all-start.4 = ((bf16[32,20,384]{2,1,0:T(8,128)(2,1)}), bf16[32,20,384]{2,1,0:T(8,128)(2,1)S(1)}, u32[]{:S(2)}, u32[]{:S(2)}) async-start(bf16[32,20,384]{2,1,0:T(8,128)(2,1)} %reshape.218), calls=%async_computation.5 | async-start | bytes 1179648 | tf_op jit(solution)/shard_map/all_to_all | solution.py:32
  339.1 4.6 %fusion.3 = bf16[320,5120]{1,0:T(8,128)(2,1)} fusion(bf16[320,128]{1,0:T(8,128)(2,1)S(1)} %reshape.211, bf16[128,5120]{1,0:T(8,128)(2,1)S(1)} %copy-done.4, bf16[320,5120]{1,0:T(8,128)(2,1)} %copy-done.1), kind=kOutput, calls=%fused_computation.13 | convolution fusion | flops 424345600 | bytes 7946240 | tf_op jit(solution)/shard_map/dot_general | solution.py:219
  343.7 13.0 %all-to-all-done.4 = bf16[32,20,384]{2,1,0:T(8,128)(2,1)S(1)} async-done(((bf16[32,20,384]{2,1,0:T(8,128)(2,1)}), bf16[32,20,384]{2,1,0:T(8,128)(2,1)S(1)}, u32[]{:S(2)}, u32[]{:S(2)}) %all-to-all-start.4) | async-done | bytes 491552 | tf_op jit(solution)/shard_map/all_to_all | solution.py:32
  356.7 0.7 convert_reduce_fusion
  (51 shorter events, 1.5 us)
Async XLA Ops:
  7.2 145.8 %copy-start = (bf16[128,5120]{1,0:T(8,128)(2,1)S(1)}, bf16[128,5120]{1,0:T(8,128)(2,1)}, u32[]{:S(2)}) copy-start(bf16[128,5120]{1,0:T(8,128)(2,1)} %param.17) | copy-start | bytes 3932164
  7.2 18.8 %copy-start.6 = (bf16[2,4,40,128]{3,2,1,0:T(8,128)(2,1)S(1)}, bf16[2,4,40,128]{3,2,1,0:T(8,128)(2,1)}, u32[]{:S(2)}) copy-start(bf16[2,4,40,128]{3,2,1,0:T(8,128)(2,1)} %param.10) | copy-start | bytes 245764
  7.2 127.5 %all-gather.3.cloned.1.call-start = ((), (), s32[]{:S(2)}) async-start(), calls=%async_computation.7 | async-start | bytes 9474048 | tf_op jit(solution)/shard_map/all_gather | solution.py:20
  8.7 17.2 %collective-permute-start = (bf16[2,4,40,128]{3,2,1,0:T(8,128)(2,1)}, bf16[2,4,40,128]{3,2,1,0:T(8,128)(2,1)S(1)}, u32[]{:S(2)}, u32[]{:S(2)}) collective-permute-start(bf16[2,4,40,128]{3,2,1,0:T(8,128)(2,1)} %param.10), channel_id=1, source_target_pairs={{0,1},{1,2},{2,3},{3,4},{4,5},{5,6},{6,7},{7,8},{8,9},{9,10},{10,1... | collective-permute-start | bytes 245768 | tf_op jit(solution)/shard_map/ppermute | solution.py:14
  13.3 13.0 %copy-start.5 = (bf16[3,3,3,128,128]{4,3,2,1,0:T(8,128)(2,1)S(1)}, bf16[3,3,3,128,128]{4,3,2,1,0:T(8,128)(2,1)}, u32[]{:S(2)}) copy-start(bf16[3,3,3,128,128]{4,3,2,1,0:T(8,128)(2,1)} %param.11) | copy-start | bytes 2654212
  17.4 145.0 %all-to-all-start.2 = ((bf16[2,160,128]{2,0,1:T(2,128)(2,1)}), bf16[2,160,128]{2,0,1:T(2,128)(2,1)S(1)}, u32[]{:S(2)}, u32[]{:S(2)}) async-start(bf16[2,160,128]{2,0,1:T(2,128)(2,1)} %copy.45), calls=%async_computation.2 | async-start | bytes 163840 | tf_op jit(solution)/shard_map/all_to_all | solution.py:212
  34.7 112.5 %copy-start.8 = (f32[5120]{0:T(1024)S(1)}, f32[5120]{0:T(1024)}, u32[]{:S(2)}) copy-start(f32[5120]{0:T(1024)} %param.13) | copy-start | bytes 61444
  153.0 3.3 copy-start.7
  156.2 5.3 %copy-start.1 = (bf16[320,5120]{1,0:T(8,128)(2,1)}, bf16[320,5120]{1,0:T(8,128)(2,1)S(1)}, u32[]{:S(2)}) copy-start(bf16[320,5120]{1,0:T(8,128)(2,1)S(1)} %get-tuple-element.36) | copy-start | bytes 9830404
  162.4 17.8 %all-to-all-start = ((bf16[2,160,384]{2,0,1:T(2,128)(2,1)}), bf16[2,160,384]{2,0,1:T(2,128)(2,1)S(1)}, u32[]{:S(2)}, u32[]{:S(2)}) async-start(bf16[2,160,384]{2,0,1:T(2,128)(2,1)} %copy.36), calls=%async_computation | async-start | bytes 491520 | tf_op jit(solution)/shard_map/all_to_all | solution.py:209
  169.5 160.4 %reduce-scatter.2.cloned.1.call-start = ((), (), s32[]{:S(2)}) async-start(), calls=%async_computation.6 | async-start | bytes 4423680 | tf_op jit(solution)/shard_map/reduce_scatter | solution.py:238
  200.2 5.3 %copy-start.2 = (bf16[320,5120]{1,0:T(8,128)(2,1)S(1)}, bf16[320,5120]{1,0:T(8,128)(2,1)}, u32[]{:S(2)}) copy-start(bf16[320,5120]{1,0:T(8,128)(2,1)} %copy-done.1) | copy-start | bytes 9830404
  200.2 5.3 %copy-start.3 = (bf16[2,4,40,5120]{3,2,1,0:T(8,128)(2,1)S(1)}, bf16[2,4,40,5120]{3,2,1,0:T(8,128)(2,1)}, u32[]{:S(2)}) copy-start(bf16[2,4,40,5120]{3,2,1,0:T(8,128)(2,1)} %param.19) | copy-start | bytes 9830404
  215.2 123.9 %copy-start.4 = (bf16[128,5120]{1,0:T(8,128)(2,1)S(1)}, bf16[128,5120]{1,0:T(8,128)(2,1)}, u32[]{:S(2)}) copy-start(bf16[128,5120]{1,0:T(8,128)(2,1)} %param.18) | copy-start | bytes 3932164
  216.2 115.7 %all-to-all-start.1 = ((bf16[64,5,128]{2,1,0:T(8,128)(2,1)}), bf16[64,5,128]{2,1,0:T(8,128)(2,1)S(1)}, u32[]{:S(2)}, u32[]{:S(2)}) async-start(bf16[64,5,128]{2,1,0:T(8,128)(2,1)} %copy.43), calls=%async_computation.1 | async-start | bytes 262144 | tf_op jit(solution)/shard_map/all_to_all | solution.py:211
  331.9 24.8 %all-to-all-start.4 = ((bf16[32,20,384]{2,1,0:T(8,128)(2,1)}), bf16[32,20,384]{2,1,0:T(8,128)(2,1)S(1)}, u32[]{:S(2)}, u32[]{:S(2)}) async-start(bf16[32,20,384]{2,1,0:T(8,128)(2,1)} %reshape.218), calls=%async_computation.5 | async-start | bytes 1179648 | tf_op jit(solution)/shard_map/all_to_all | solution.py:32
Sparse Core Ops, SparseCore 0:
  12.3 122.3 all-gather.2
  215.4 114.5 reduce-scatter.1
where the time goes:
time: 365 us; the launch traced here: 364 us
  waiting for transfers between devices  233 us (64%)
  matrix products  46.7 us (13%)
  starting transfers between devices  31.3 us (9%)
  local copies, waits for them, and re-layouts  17.8 us (5%)
  blocking collectives  17.4 us (5%)
  between operations  14.5 us (4%)
    reduce_scatter x1, waiting for transfers between devices, shards(): lax.psum_scatter(part_spatial.astype(jnp.bfloat16), 'dp', scatter_dimensi...  110 us
    all_gather x1, waiting for transfers between devices, side_by_side(): whole = lax.all_gather(both, axis, axis=dim, tiled=True)  100 us
    all_to_all x1, blocking collectives, shards(): lax.all_to_all(grad_packed_patched, 'ts', split_axis=0, concat_axis=1, ti...  17.4 us
    all_to_all x1, waiting for transfers between devices, sum_at_owner(): lax.all_to_all(parts, axis, split_axis=0, concat_axis=0, tiled=True)  13 us
    unnamed x19, local copies, waits for them, and re-layouts  12.5 us
    all_to_all x1, waiting for transfers between devices, shards(): lax.all_to_all(packed_two, 'ts', split_axis=1, concat_axis=0, tiled=True)  10.6 us
    all_to_all x1, starting transfers between devices, shards(): lax.all_to_all(grad_mix_two, 'ts', split_axis=1, concat_axis=0, tiled=True)  8.51 us
  transfers between devices with their start and end apart: 7, of which 4 were waited for; matrix products, arithmetic and copies ran while one was open for 13% of the time, Pallas kernels for 0%

commit v1 on v0

--- a/solution.py
+++ b/solution.py
@@ -209,7 +209,10 @@
     patched = lax.all_to_all(packed_two, "ts", split_axis=1, concat_axis=0, tiled=True)
     mixture_patched, attend_two = clip_forward(patched)
     mixture_two = lax.all_to_all(mixture_patched, "ts", split_axis=0, concat_axis=1, tiled=True)
-    grad_patched = lax.all_to_all(grad_mix_two, "ts", split_axis=1, concat_axis=0, tiled=True)
+    grad_patched = jnp.concatenate(
+        lax.all_to_all(jnp.stack(jnp.split(grad_mix_two, lax.axis_size("ts"), axis=1)), "ts", 0, 0),
+        axis=0,
+    )
     grad_packed_patched = clip_backward(patched, attend_two, grad_patched)
     grad_packed_two = lax.all_to_all(
         grad_packed_patched, "ts", split_axis=0, concat_axis=1, tiled=True

time: 365 us -> 365 us (level)
  local copies, waits for them, and re-layouts: 17.8 us -> 36 us
  waiting for transfers between devices: 233 us -> 215 us
    unnamed x19 -> x50, local copies, waits for them, and re-layouts: 12.5 us -> 30.7 us
    all_gather x1, waiting for transfers between devices: 100 us -> 81.9 us  [side_by_side(): whole = lax.all_gather(both, axis, axis=dim, tiled=True)]
  transfers between devices with their start and end apart: 7 -> 7, of which waited for: 4 -> 4; matrix products, arithmetic and copies ran while one was open for 13% -> 18% of each run, Pallas kernels for 0% -> 0%
where the time goes in v1:
time: 365 us; the launch traced here: 364 us
  waiting for transfers between devices  215 us (59%)
  matrix products  46.7 us (13%)
  local copies, waits for them, and re-layouts  36 us (10%)
  starting transfers between devices  31.3 us (9%)
  blocking collectives  17.4 us (5%)
  between operations  14.5 us (4%)
    reduce_scatter x1, waiting for transfers between devices, shards(): lax.psum_scatter(part_spatial.astype(jnp.bfloat16), 'dp', scatter_dimensi...  110 us
    all_gather x1, waiting for transfers between devices, side_by_side(): whole = lax.all_gather(both, axis, axis=dim, tiled=True)  81.9 us
    unnamed x50, local copies, waits for them, and re-layouts  30.7 us
    all_to_all x1, blocking collectives, shards(): lax.all_to_all(grad_packed_patched, 'ts', split_axis=0, concat_axis=1, ti...  17.4 us
    all_to_all x1, waiting for transfers between devices, sum_at_owner(): lax.all_to_all(parts, axis, split_axis=0, concat_axis=0, tiled=True)  13 us
    all_to_all x1, waiting for transfers between devices, shards(): lax.all_to_all(packed_two, 'ts', split_axis=1, concat_axis=0, tiled=True)  10.6 us
    all_to_all x1, starting transfers between devices, shards(): lax.all_to_all(jnp.stack(jnp.split(grad_mix_two, lax.axis_size('ts'), axi...  8.51 us
  transfers between devices with their start and end apart: 7, of which 4 were waited for; matrix products, arithmetic and copies ran while one was open for 18% of the time, Pallas kernels for 0%

profile of v1, /device:TPU:1, one launch (start us, length us, event | category | flops | bytes accessed | tf_op | source)
XLA Modules:
  0.0 364.4 jit_solution(16975596645708631721)
XLA Ops:
  7.2 1.5 maximum_bitcast_fusion
  8.7 4.6 %collective-permute-start = (bf16[2,4,40,128]{3,2,1,0:T(8,128)(2,1)}, bf16[2,4,40,128]{3,2,1,0:T(8,128)(2,1)S(1)}, u32[]{:S(2)}, u32[]{:S(2)}) collective-permute-start(bf16[2,4,40,128]{3,2,1,0:T(8,128)(2,1)} %param.10), channel_id=1, source_target_pairs={{0,1},{1,2},{2,3},{3,4},{4,5},{5,6},{6,7},{7,8},{8,9},{9,10},{10,1... | collective-permute-start | bytes 245768 | tf_op jit(solution)/shard_map/ppermute | solution.py:14
  13.3 3.4 convolution_convert_fusion.2
  16.7 0.6 constant_dynamic-update-slice_fusion.31
  17.3 0.6 constant_dynamic-update-slice_fusion.30
  17.9 0.6 constant_dynamic-update-slice_fusion.29
  18.5 0.6 constant_dynamic-update-slice_fusion.28
  19.1 0.6 constant_dynamic-update-slice_fusion.27
  19.7 0.6 constant_dynamic-update-slice_fusion.26
  20.3 0.6 constant_dynamic-update-slice_fusion.25
  20.9 0.6 constant_dynamic-update-slice_fusion.24
  21.5 0.6 constant_dynamic-update-slice_fusion.23
  22.0 0.5 constant_dynamic-update-slice_fusion.22
  22.6 0.6 constant_dynamic-update-slice_fusion.21
  23.2 0.6 constant_dynamic-update-slice_fusion.20
  23.8 0.6 constant_dynamic-update-slice_fusion.19
  24.4 0.6 constant_dynamic-update-slice_fusion.18
  25.0 0.6 constant_dynamic-update-slice_fusion.17
  25.6 0.6 constant_dynamic-update-slice_fusion.16
  26.2 0.6 constant_dynamic-update-slice_fusion.15
  26.8 0.6 constant_dynamic-update-slice_fusion.14
  27.4 0.6 constant_dynamic-update-slice_fusion.13
  28.0 0.6 constant_dynamic-update-slice_fusion.12
  28.5 0.6 constant_dynamic-update-slice_fusion.11
  29.1 0.6 constant_dynamic-update-slice_fusion.10
  29.7 0.6 constant_dynamic-update-slice_fusion.9
  30.3 0.6 constant_dynamic-update-slice_fusion.8
  30.9 0.6 constant_dynamic-update-slice_fusion.7
  31.5 0.6 constant_dynamic-update-slice_fusion.6
  32.1 0.6 constant_dynamic-update-slice_fusion.5
  32.7 0.6 constant_dynamic-update-slice_fusion.4
  33.3 0.6 constant_dynamic-update-slice_fusion.3
  33.8 0.6 constant_dynamic-update-slice_fusion.2
  34.4 0.6 constant_dynamic-update-slice_fusion.1
  35.0 0.6 constant_dynamic-update-slice_fusion
  35.6 8.5 %all-to-all-start.2 = ((bf16[32,2,5,128]{3,1,2,0:T(2,128)(2,1)}), bf16[32,2,5,128]{3,1,2,0:T(2,128)(2,1)S(1)}, u32[]{:S(2)}, u32[]{:S(2)}) async-start(bf16[32,2,5,128]{3,1,2,0:T(2,128)(2,1)} %constant_dynamic-update-slice_fusion), calls=%async_computation.2 | async-start | bytes 163840 | tf_op jit(solution)/shard_map/all_to_all | solution.py:213
  48.7 4.2 %fusion.4 = (f32[320]{0:T(512)S(1)}, bf16[320,5120]{1,0:T(8,128)(2,1)}) fusion(bf16[128,5120]{1,0:T(8,128)(2,1)} %param.12, f32[320,128]{1,0:T(8,128)S(1)} %convolution_add_fusion.1, bf16[320,128]{1,0:T(8,128)(2,1)S(1)} %bitcast.369, bf16[3,3,3,128,128]{4,3,2,1,0:T(8,128)(2,1)S(1)} %copy-done.5), kind=kOutput, calls=%fused_computation.15 | convolution fusion | flops 436879040 | bytes 4867328 | tf_op jit(solution)/shard_map/dot_general | solution.py:184
  52.9 81.9 %all-gather.3.cloned.1.call-done = bf16[256,20,768]{2,1,0:T(8,128)(2,1)} async-done(((bf16[1,20,768]{2,1,0:T(8,128)(2,1)}), bf16[256,20,768]{2,1,0:T(8,128)(2,1)}) %all-gather.3.cloned.1.call-update) | async-done | bytes 7864336 | tf_op jit(solution)/shard_map/all_gather | solution.py:20
  134.8 12.5 %reshape.215 = bf16[5120,768]{1,0:T(8,128)(2,1)} reshape(bf16[256,20,768]{2,1,0:T(8,128)(2,1)} %all-gather.3.cloned.1.call-done) | data formatting | bytes 15728640
  147.3 5.0 %fusion.26 = bf16[320,384]{1,0:T(8,128)(2,1)S(1)} fusion(bf16[5120,768]{1,0:T(8,128)(2,1)} %reshape.215, bf16[320,5120]{1,0:T(8,128)(2,1)} %get-tuple-element.64, f32[5120]{0:T(1024)S(1)} %copy-done.8, f32[320]{0:T(512)S(1)} %add_rsqrt_fusion.1), kind=kOutput, calls=%fused_computation.35 | convolution fusion | flops 1264967680 | bytes 7476480 | tf_op jit(solution)/shard_map/dot_general | solution.py:188
  152.3 0.3 fusion.184
  152.6 0.5 convolution_convert_fusion.6
  153.1 3.3 fusion.7
  156.4 5.2 %fusion.29 = bf16[320,384]{1,0:T(8,128)(2,1)S(1)} fusion(bf16[5120,768]{1,0:T(8,128)(2,1)} %reshape.215, bf16[320,5120]{1,0:T(8,128)(2,1)S(1)} %get-tuple-element.68, f32[5120]{0:T(1024)S(1)} %copy-done.7, f32[320]{0:T(512)S(1)} %get-tuple-element.62), kind=kOutput, calls=%fused_computation.36 | convolution fusion | flops 1264967680 | bytes 7476480 | tf_op jit(solution)/shard_map/dot_general | solution.py:200
  161.6 0.9 copy.66
  162.5 7.1 %all-to-all-start = ((bf16[2,160,384]{2,0,1:T(2,128)(2,1)}), bf16[2,160,384]{2,0,1:T(2,128)(2,1)S(1)}, u32[]{:S(2)}, u32[]{:S(2)}) async-start(bf16[2,160,384]{2,0,1:T(2,128)(2,1)} %copy.66), calls=%async_computation | async-start | bytes 491520 | tf_op jit(solution)/shard_map/all_to_all | solution.py:209
  169.8 10.6 %all-to-all-done = bf16[2,160,384]{2,0,1:T(2,128)(2,1)S(1)} async-done(((bf16[2,160,384]{2,0,1:T(2,128)(2,1)}), bf16[2,160,384]{2,0,1:T(2,128)(2,1)S(1)}, u32[]{:S(2)}, u32[]{:S(2)}) %all-to-all-start) | async-done | bytes 245792 | tf_op jit(solution)/shard_map/all_to_all | solution.py:209
  180.9 0.8 fusion.189
  182.7 17.4 %all_to_all.55 = bf16[64,5,384]{2,1,0:T(8,128)(2,1)S(1)} all-to-all(bf16[64,5,384]{2,1,0:T(8,128)(2,1)S(1)} %copy.114), channel_id=1, replica_groups=mesh['dp'=8,'ts'=32] {'ts'}, dimensions={0} | all-to-all | bytes 491520 | tf_op jit(solution)/shard_map/all_to_all | solution.py:217
  200.3 5.3 %fusion.14 = (f32[320]{0:T(512)S(1)}, f32[320,5120]{1,0:T(8,128)S(1)}) fusion(bf16[320,5120]{1,0:T(8,128)(2,1)} %copy-done.1, f32[5120]{0:T(1024)S(1)} %copy-done.7, bf16[320,384]{1,0:T(8,128)(2,1)S(1)} %reshape.211, bf16[5120,768]{1,0:T(8,128)(2,1)} %reshape.215), kind=kOutput, calls=%fused_computation.25 | convolution fusion | flops 1264844544 | bytes 14030080 | tf_op jit(solution)/shard_map/dot_general | solution.py:227
  205.6 2.0 fusion.41
  207.6 0.4 convolution_convert_fusion.4
  208.0 0.2 multiply_reduce_fusion
  208.5 0.3 fusion.39
  208.7 6.6 %convolution_convert_fusion = bf16[5120,384]{1,0:T(8,128)(2,1)} fusion(bf16[320,5120]{1,0:T(8,128)(2,1)} %get-tuple-element.64, f32[5120]{0:T(1024)S(1)} %copy-done.8, f32[320]{0:T(512)S(1)} %add_rsqrt_fusion.1, bf16[320,128]{1,0:T(8,128)(2,1)S(1)} %bitcast.376, bf16[320,128]{1,0:T(8,128)(2,1)S(1)} %bitcast.377, bf16[320,128]{1,0:T(8,128)(2,1)S(1)} %bitcast.366), kind=kOutput, calls=%fused_computation.11 | convolution fusion | flops 1267548160 | bytes 7476480 | tf_op jit(solution)/shard_map/dot_general | solution.py:238
  215.3 0.2 fusion.46
  215.6 0.7 copy.73
  216.3 4.0 %all-to-all-start.1 = ((bf16[64,5,128]{2,1,0:T(8,128)(2,1)}), bf16[64,5,128]{2,1,0:T(8,128)(2,1)S(1)}, u32[]{:S(2)}, u32[]{:S(2)}) async-start(bf16[64,5,128]{2,1,0:T(8,128)(2,1)} %copy.73), calls=%async_computation.1 | async-start | bytes 262144 | tf_op jit(solution)/shard_map/all_to_all | solution.py:211
  220.3 109.8 %reduce-scatter.2.cloned.1.call-done = bf16[640,384]{1,0:T(8,128)(2,1)} async-done(((bf16[5120,384]{1,0:T(8,128)(2,1)}), bf16[640,384]{1,0:T(8,128)(2,1)}) %reduce-scatter.2.cloned.1.call-update) | async-done | bytes 491536 | tf_op jit(solution)/shard_map/reduce_scatter | solution.py:241
  330.1 1.9 reshape.213
  332.0 7.0 %all-to-all-start.4 = ((bf16[32,20,384]{2,1,0:T(8,128)(2,1)}), bf16[32,20,384]{2,1,0:T(8,128)(2,1)S(1)}, u32[]{:S(2)}, u32[]{:S(2)}) async-start(bf16[32,20,384]{2,1,0:T(8,128)(2,1)} %reshape.213), calls=%async_computation.5 | async-start | bytes 1179648 | tf_op jit(solution)/shard_map/all_to_all | solution.py:32
  339.2 4.6 %fusion.3 = bf16[320,5120]{1,0:T(8,128)(2,1)} fusion(bf16[320,128]{1,0:T(8,128)(2,1)S(1)} %reshape.207, bf16[128,5120]{1,0:T(8,128)(2,1)S(1)} %copy-done.4, bf16[320,5120]{1,0:T(8,128)(2,1)} %copy-done.1), kind=kOutput, calls=%fused_computation.13 | convolution fusion | flops 424345600 | bytes 7946240 | tf_op jit(solution)/shard_map/dot_general | solution.py:222
  343.8 13.0 %all-to-all-done.4 = bf16[32,20,384]{2,1,0:T(8,128)(2,1)S(1)} async-done(((bf16[32,20,384]{2,1,0:T(8,128)(2,1)}), bf16[32,20,384]{2,1,0:T(8,128)(2,1)S(1)}, u32[]{:S(2)}, u32[]{:S(2)}) %all-to-all-start.4) | async-done | bytes 491552 | tf_op jit(solution)/shard_map/all_to_all | solution.py:32
  356.8 0.7 convert_reduce_fusion
  (84 shorter events, 6.8 us)
Async XLA Ops:
  7.2 145.9 %copy-start = (bf16[128,5120]{1,0:T(8,128)(2,1)S(1)}, bf16[128,5120]{1,0:T(8,128)(2,1)}, u32[]{:S(2)}) copy-start(bf16[128,5120]{1,0:T(8,128)(2,1)} %param.17) | copy-start | bytes 3932164
  7.2 37.0 %copy-start.6 = (bf16[2,4,40,128]{3,2,1,0:T(8,128)(2,1)S(1)}, bf16[2,4,40,128]{3,2,1,0:T(8,128)(2,1)}, u32[]{:S(2)}) copy-start(bf16[2,4,40,128]{3,2,1,0:T(8,128)(2,1)} %param.10) | copy-start | bytes 245764
  7.2 127.6 %all-gather.3.cloned.1.call-start = ((), (), s32[]{:S(2)}) async-start(), calls=%async_computation.7 | async-start | bytes 9474048 | tf_op jit(solution)/shard_map/all_gather | solution.py:20
  8.7 35.4 %collective-permute-start = (bf16[2,4,40,128]{3,2,1,0:T(8,128)(2,1)}, bf16[2,4,40,128]{3,2,1,0:T(8,128)(2,1)S(1)}, u32[]{:S(2)}, u32[]{:S(2)}) collective-permute-start(bf16[2,4,40,128]{3,2,1,0:T(8,128)(2,1)} %param.10), channel_id=1, source_target_pairs={{0,1},{1,2},{2,3},{3,4},{4,5},{5,6},{6,7},{7,8},{8,9},{9,10},{10,1... | collective-permute-start | bytes 245768 | tf_op jit(solution)/shard_map/ppermute | solution.py:14
  13.3 31.2 %copy-start.5 = (bf16[3,3,3,128,128]{4,3,2,1,0:T(8,128)(2,1)S(1)}, bf16[3,3,3,128,128]{4,3,2,1,0:T(8,128)(2,1)}, u32[]{:S(2)}) copy-start(bf16[3,3,3,128,128]{4,3,2,1,0:T(8,128)(2,1)} %param.11) | copy-start | bytes 2654212
  35.6 126.9 %all-to-all-start.2 = ((bf16[32,2,5,128]{3,1,2,0:T(2,128)(2,1)}), bf16[32,2,5,128]{3,1,2,0:T(2,128)(2,1)S(1)}, u32[]{:S(2)}, u32[]{:S(2)}) async-start(bf16[32,2,5,128]{3,1,2,0:T(2,128)(2,1)} %constant_dynamic-update-slice_fusion), calls=%async_computation.2 | async-start | bytes 163840 | tf_op jit(solution)/shard_map/all_to_all | solution.py:213
  52.9 94.4 %copy-start.8 = (f32[5120]{0:T(1024)S(1)}, f32[5120]{0:T(1024)}, u32[]{:S(2)}) copy-start(f32[5120]{0:T(1024)} %param.13) | copy-start | bytes 61444
  153.1 3.3 copy-start.7
  156.3 5.2 %copy-start.1 = (bf16[320,5120]{1,0:T(8,128)(2,1)}, bf16[320,5120]{1,0:T(8,128)(2,1)S(1)}, u32[]{:S(2)}) copy-start(bf16[320,5120]{1,0:T(8,128)(2,1)S(1)} %get-tuple-element.68) | copy-start | bytes 9830404
  162.5 17.9 %all-to-all-start = ((bf16[2,160,384]{2,0,1:T(2,128)(2,1)}), bf16[2,160,384]{2,0,1:T(2,128)(2,1)S(1)}, u32[]{:S(2)}, u32[]{:S(2)}) async-start(bf16[2,160,384]{2,0,1:T(2,128)(2,1)} %copy.66), calls=%async_computation | async-start | bytes 491520 | tf_op jit(solution)/shard_map/all_to_all | solution.py:209
  169.6 160.5 %reduce-scatter.2.cloned.1.call-start = ((), (), s32[]{:S(2)}) async-start(), calls=%async_computation.6 | async-start | bytes 4423680 | tf_op jit(solution)/shard_map/reduce_scatter | solution.py:241
  200.3 5.3 %copy-start.2 = (bf16[320,5120]{1,0:T(8,128)(2,1)S(1)}, bf16[320,5120]{1,0:T(8,128)(2,1)}, u32[]{:S(2)}) copy-start(bf16[320,5120]{1,0:T(8,128)(2,1)} %copy-done.1) | copy-start | bytes 9830404
  200.3 5.3 %copy-start.3 = (bf16[2,4,40,5120]{3,2,1,0:T(8,128)(2,1)S(1)}, bf16[2,4,40,5120]{3,2,1,0:T(8,128)(2,1)}, u32[]{:S(2)}) copy-start(bf16[2,4,40,5120]{3,2,1,0:T(8,128)(2,1)} %param.19) | copy-start | bytes 9830404
  215.3 123.9 %copy-start.4 = (bf16[128,5120]{1,0:T(8,128)(2,1)S(1)}, bf16[128,5120]{1,0:T(8,128)(2,1)}, u32[]{:S(2)}) copy-start(bf16[128,5120]{1,0:T(8,128)(2,1)} %param.18) | copy-start | bytes 3932164
  216.3 115.7 %all-to-all-start.1 = ((bf16[64,5,128]{2,1,0:T(8,128)(2,1)}), bf16[64,5,128]{2,1,0:T(8,128)(2,1)S(1)}, u32[]{:S(2)}, u32[]{:S(2)}) async-start(bf16[64,5,128]{2,1,0:T(8,128)(2,1)} %copy.73), calls=%async_computation.1 | async-start | bytes 262144 | tf_op jit(solution)/shard_map/all_to_all | solution.py:211
  332.0 24.8 %all-to-all-start.4 = ((bf16[32,20,384]{2,1,0:T(8,128)(2,1)}), bf16[32,20,384]{2,1,0:T(8,128)(2,1)S(1)}, u32[]{:S(2)}, u32[]{:S(2)}) async-start(bf16[32,20,384]{2,1,0:T(8,128)(2,1)} %reshape.213), calls=%async_computation.5 | async-start | bytes 1179648 | tf_op jit(solution)/shard_map/all_to_all | solution.py:32
Sparse Core Ops, SparseCore 0:
  12.3 122.4 all-gather.2
  215.4 114.6 reduce-scatter.1
